TPU v7x, 32 devices: a whole 2x2x4 slice. The times are simulated.
32 devices in a mesh: req: 2 (over y), patch: 16 (over z, x, core).
Axes of the slice: x: 2, y: 2, z: 4, core: 2. Of those that a mesh axis runs over, the one named last changes fastest.
Arguments:
- tokens: bfloat16 [1536, 1152], P(('req', 'patch')), parts along dimension 0, may hold values from -6 to 6
- positions: int32 [2, 1536], P(None, ('req', 'patch')), parts along dimension 1, may hold values from 0 to 95
- counts: int32 [32], P('req'), parts along dimension 0, may hold values from 1 to 48, 384 in all
- timestep: int32 [2], P('req'), parts along dimension 0, may hold values from 0 to 999
- time_in: bfloat16 [256, 1152], replicated, may hold values from -0.375 to 0.375
- time_out: bfloat16 [1152, 1152], P(None, 'patch'), may hold values from -0.1875 to 0.1875
- ada_weight: bfloat16 [1152, 3456], P('patch'), may hold values from -0.375 to 0.375
- qkv_weight: bfloat16 [1152, 3456], replicated, may hold values from -2 to 2, as said below
- out_weight: bfloat16 [1152, 1152], replicated, may hold values from -0.1875 to 0.1875
Outputs:
- block_out: bfloat16 [1536, 1152], P(('req', 'patch')), parts along dimension 0
There are 2 independent parts, one for each index of `req`. A program takes and returns all parts, laid end to end along the dimension named above; an argument that names none is the same for every part. Nothing has to cross between parts.
Inputs may be any that keep to these rules, and one draw needn't show every extreme that they name: `counts`: used slots are the first ones of each block; they sum to exactly 384, and some block uses all 48. `qkv_weight`: columns are 1152 of queries, 1152 of keys, 1152 of values, each head's 72 columns side by side.
All inputs are finite; a program needn't handle non-finite values.
Results may differ from a plain program's by a relative error of at most 0.0039.
Values may be sent and summed in bfloat16 or wider, within the bound.
A program may use at most 64 MiB of HBM per device.

v0:
```python
import math

import jax
import jax.numpy as jnp
from jax import lax
from jax.sharding import PartitionSpec as P

HEADS = 16


neg_large = -1e30
key_block = 512


def time_features(timestep, freq_size):
    half_size = freq_size // 2
    frequencies = jnp.exp(-math.log(10000.0) * jnp.arange(half_size, dtype=jnp.float32) / half_size)
    angles = timestep.astype(jnp.float32)[:, None] * frequencies[None, :]
    return jnp.concatenate([jnp.cos(angles), jnp.sin(angles)], axis=1).astype(jnp.bfloat16)


def position_table(positions, model_width):
    quarter = model_width // 4
    omegas = jnp.power(10000.0, -jnp.arange(quarter, dtype=jnp.float32) / quarter)
    row_angle = positions[0].astype(jnp.float32)[:, None] * omegas[None, :]
    col_angle = positions[1].astype(jnp.float32)[:, None] * omegas[None, :]
    return jnp.concatenate(
        [jnp.sin(row_angle), jnp.cos(row_angle), jnp.sin(col_angle), jnp.cos(col_angle)], axis=1
    )


def attend_update(running, query_heads, key_piece, value_piece, mask_piece, inv_root):
    row_top, denominator, weighted = running
    key_count = key_piece.shape[0]
    head_count = query_heads.shape[1]
    head_size = query_heads.shape[2]
    key_heads = key_piece.reshape(key_count, head_count, head_size)
    value_heads = value_piece.reshape(key_count, head_count, head_size)
    scores = (
        jnp.einsum("qhd,khd->hqk", query_heads, key_heads, preferred_element_type=jnp.float32)
        * inv_root
    )
    scores = jnp.where(mask_piece[None, None, :], scores, neg_large)
    new_top = jnp.maximum(row_top, jnp.max(scores, axis=2))
    weights = jnp.where(mask_piece[None, None, :], jnp.exp(scores - new_top[:, :, None]), 0.0)
    factor = jnp.exp(row_top - new_top)
    denominator = denominator * factor + jnp.sum(weights, axis=2)
    rounded = weights.astype(jnp.bfloat16)
    weighted = weighted * factor[:, :, None] + jnp.einsum(
        "hqk,khd->hqd", rounded, value_heads, preferred_element_type=jnp.float32
    )
    return (new_top, denominator, weighted)


def make_folder(query_heads, key_valid, inv_root):

    def fold_keys(running, shard_piece, start_row):
        key_piece, value_piece = shard_piece
        key_count = key_piece.shape[0]
        if key_count > 2 * key_block and key_count % key_block == 0:
            block_total = key_count // key_block

            def block_step(carried, block_items):
                return (
                    attend_update(
                        carried,
                        query_heads,
                        block_items[0],
                        block_items[1],
                        block_items[2],
                        inv_root,
                    ),
                    None,
                )

            stacked = (
                key_piece.reshape(block_total, key_block, key_piece.shape[1]),
                value_piece.reshape(block_total, key_block, value_piece.shape[1]),
                key_valid.reshape(block_total, key_block),
            )
            running, unused = lax.scan(block_step, running, stacked)
            return running
        return attend_update(running, query_heads, key_piece, value_piece, key_valid, inv_root)

    return fold_keys


def initial_state(query_rows, head_count, head_size):
    return (
        jnp.full((head_count, query_rows), neg_large, jnp.float32),
        jnp.zeros((head_count, query_rows), jnp.float32),
        jnp.zeros((head_count, query_rows, head_size), jnp.float32),
    )


def finish_state(running):
    row_top, denominator, weighted = running
    normalized = weighted / denominator[:, :, None]
    head_count, query_rows, head_size = normalized.shape
    return (
        jnp.transpose(normalized, (1, 0, 2))
        .reshape(query_rows, head_count * head_size)
        .astype(jnp.bfloat16)
    )


def per_device(
    tokens, positions, counts, timestep, time_in, time_out, ada_weight, qkv_weight, out_weight
):
    devices = lax.axis_size("patch")
    my_index = lax.axis_index("patch")
    local_rows = tokens.shape[0]
    model_width = tokens.shape[1]
    head_count = HEADS
    head_size = model_width // head_count
    inv_root = 1.0 / math.sqrt(head_size)
    features = time_features(timestep, time_in.shape[0])
    hidden_time = jax.nn.silu(
        jnp.dot(features, time_in, preferred_element_type=jnp.float32)
    ).astype(jnp.bfloat16)
    cond_part = jnp.dot(hidden_time, time_out, preferred_element_type=jnp.float32)
    activated = jax.nn.silu(cond_part).astype(jnp.bfloat16)
    partial_mod = jnp.dot(activated, ada_weight, preferred_element_type=jnp.float32)
    modulation = lax.psum(partial_mod, "patch")
    shift_mod = modulation[:, :model_width]
    scale_mod = modulation[:, model_width : 2 * model_width]
    gate_mod = modulation[:, 2 * model_width :]
    x_in = tokens.astype(jnp.float32) + position_table(positions, model_width)
    mean_value = jnp.mean(x_in, axis=1, keepdims=True)
    centered = x_in - mean_value
    variance = jnp.mean(centered * centered, axis=1, keepdims=True)
    normed = centered * lax.rsqrt(variance + 1e-06)
    modulated = (normed * (1.0 + scale_mod) + shift_mod).astype(jnp.bfloat16)
    counts_here = lax.dynamic_index_in_dim(counts, my_index, keepdims=False)
    row_ids = jnp.arange(local_rows, dtype=jnp.int32)
    row_valid = row_ids < counts_here
    projections = jnp.dot(modulated, qkv_weight, preferred_element_type=jnp.float32).astype(
        jnp.bfloat16
    )
    groups = devices // head_count
    part_rows = local_rows // groups
    query_split = projections[:, :model_width].reshape(groups, part_rows, head_count, head_size)
    query_send = jnp.transpose(query_split, (0, 2, 1, 3)).reshape(devices, part_rows, head_size)
    key_split = projections[:, model_width : 2 * model_width].reshape(
        local_rows, head_count, head_size
    )
    value_split = projections[:, 2 * model_width :].reshape(local_rows, head_count, head_size)
    pair_heads = jnp.transpose(jnp.concatenate([key_split, value_split], axis=2), (1, 0, 2))
    pair_send = jnp.broadcast_to(pair_heads[None], (groups, head_count, local_rows, 2 * head_size))
    pair_send = pair_send.reshape(devices, local_rows, 2 * head_size)
    got_query, got_pair = (
        lax.all_to_all(query_send, "patch", split_axis=0, concat_axis=0, tiled=True),
        lax.all_to_all(pair_send, "patch", split_axis=0, concat_axis=0, tiled=True),
    )
    query_rows = devices * part_rows
    query_heads = got_query.reshape(query_rows, 1, head_size)
    all_pairs = got_pair.reshape(devices * local_rows, 2 * head_size)
    key_valid = (jnp.arange(local_rows, dtype=jnp.int32)[None, :] < counts[:, None]).reshape(-1)
    folder = make_folder(query_heads, key_valid, inv_root)
    running = folder(
        initial_state(query_rows, 1, head_size),
        (all_pairs[:, :head_size], all_pairs[:, head_size:]),
        0,
    )
    head_result = finish_state(running).reshape(devices, part_rows, head_size)
    came_back = lax.all_to_all(head_result, "patch", split_axis=0, concat_axis=0, tiled=True)
    attended = jnp.transpose(
        came_back.reshape(groups, head_count, part_rows, head_size), (0, 2, 1, 3)
    )
    attended = attended.reshape(local_rows, model_width)
    projected = jnp.dot(attended, out_weight, preferred_element_type=jnp.float32)
    valid_column = row_valid.astype(jnp.float32)[:, None]
    return (x_in + gate_mod * projected * valid_column).astype(jnp.bfloat16)


def solution(mesh):
    placed = (
        P(("req", "patch"), None),
        P(None, ("req", "patch")),
        P("req"),
        P("req"),
        P(),
        P(None, "patch"),
        P("patch", None),
        P(),
        P(),
    )
    return jax.shard_map(
        per_device, mesh=mesh, in_specs=placed, out_specs=P(("req", "patch"), None), check_vma=False
    )
```

profile of v0, /device:TPU:0, one launch (start us, length us, event | category | flops | bytes accessed | tf_op | source)
XLA Modules:
  0.0 123.4 jit_solution(13335369351316423858)
XLA Ops:
  0.0 0.9 convert_bitcast_fusion
  1.6 1.0 fusion.25
  2.7 1.1 multiply_reduce_fusion
  4.5 1.3 %convolution_reduce_fusion = f32[1152]{0:T(1024)S(1)} fusion(bf16[256,1]{0,1:T(2,128)(2,1)S(1)} %reshape.180, bf16[256,1152]{1,0:T(8,128)(2,1)} %param.13), kind=kOutput, calls=%fused_computation.15 | convolution fusion | flops 589824 | bytes 594944 | tf_op jit(solution)/shard_map/dot_general | solution.py:119
  5.8 1.6 %fusion.27 = f32[1,3456]{1,0:T(1,128)S(1)} fusion(bf16[72,3456]{1,0:T(8,128)(2,1)} %param.15, bf16[1152,1]{0,1:T(2,128)(2,1)S(1)} %reshape.182, bf16[1152,72]{0,1:T(8,128)(2,1)} %param.14), kind=kOutput, calls=%fused_computation.46 | convolution fusion | flops 663912 | bytes 679680 | tf_op jit(solution)/shard_map/dot_general | solution.py:123
  7.4 63.0 %psum.7 = f32[1,3456]{1,0:T(1,128)S(1)} all-reduce(f32[1,3456]{1,0:T(1,128)S(1)} %fusion.27), channel_id=1, replica_groups=mesh['req'=2,'patch'=16] {'patch'}, use_global_device_ids=true, to_apply=%region_0.1 | all-reduce | flops 3456 | bytes 27648 | tf_op jit(solution)/shard_map/psum | solution.py:124
  70.4 4.6 %convolution_convert_fusion = bf16[48,3456]{1,0:T(8,128)(2,1)S(1)} fusion(bf16[1152,3456]{1,0:T(8,128)(2,1)} %param.16, f32[1152]{0:T(1024)S(1)} %get-tuple-element.6, f32[1152]{0:T(1024)S(1)} %get-tuple-element.7, f32[48]{0:T(128)S(1)} %add_rsqrt_fusion, f32[48]{0:T(128)S(1)} %broadcast_multiply_fusion, f32[48,1152]{1,0:T(8,128)S(1)} %concatenate.13, ...), kind=kOutput, calls=%fused_computation | convolution fusion | flops 382758912 | bytes 8635776 | tf_op jit(solution)/shard_map/dot_general | solution.py:137
  75.0 0.7 fusion.38
  76.1 0.7 copy.16
  76.8 3.5 %all-to-all-start = ((bf16[16,48,72]{2,1,0:T(8,128)(2,1)}), bf16[16,48,72]{2,1,0:T(8,128)(2,1)S(1)}, u32[]{:S(2)}, u32[]{:S(2)}) async-start(bf16[16,48,72]{2,1,0:T(8,128)(2,1)} %bitcast.38), calls=%async_computation | async-start | bytes 393216 | tf_op jit(solution)/shard_map/all_to_all | solution.py:152
  80.3 1.2 %reshape.175 = bf16[48,16,72]{2,1,0:T(8,128)(2,1)S(1)} reshape(bf16[48,1152]{1,0:T(8,128)(2,1)} %get-tuple-element.8) | data formatting | bytes 221184 | tf_op jit(solution)/shard_map/reshape | solution.py:144
  81.6 0.7 copy.11
  82.7 1.8 %maximum_bitcast_fusion = bf16[16,48,144]{2,1,0:T(8,128)(2,1)} fusion(bf16[48,16,72]{2,0,1:T(8,128)(2,1)S(1)} %copy.12, bf16[48,16,72]{2,0,1:T(8,128)(2,1)} %copy.11), kind=kLoop, calls=%fused_computation.17 | loop fusion | flops 442368 | bytes 442368 | tf_op jit(solution)/shard_map/transpose | solution.py:148
  84.5 4.7 %all-to-all-done = bf16[16,48,72]{2,1,0:T(8,128)(2,1)S(1)} async-done(((bf16[16,48,72]{2,1,0:T(8,128)(2,1)}), bf16[16,48,72]{2,1,0:T(8,128)(2,1)S(1)}, u32[]{:S(2)}, u32[]{:S(2)}) %all-to-all-start) | async-done | bytes 110624 | tf_op jit(solution)/shard_map/all_to_all | solution.py:152
  89.2 0.7 copy-done.2
  89.9 3.6 %all-to-all-start.1 = ((bf16[16,48,144]{2,1,0:T(8,128)(2,1)}), bf16[16,48,144]{2,1,0:T(8,128)(2,1)S(1)}, u32[]{:S(2)}, u32[]{:S(2)}) async-start(bf16[16,48,144]{2,1,0:T(8,128)(2,1)} %maximum_bitcast_fusion), calls=%async_computation.1 | async-start | bytes 786432 | tf_op jit(solution)/shard_map/all_to_all | solution.py:153
  93.6 12.0 %all-to-all-done.1 = bf16[16,48,144]{2,1,0:T(8,128)(2,1)S(1)} async-done(((bf16[16,48,144]{2,1,0:T(8,128)(2,1)}), bf16[16,48,144]{2,1,0:T(8,128)(2,1)S(1)}, u32[]{:S(2)}, u32[]{:S(2)}) %all-to-all-start.1) | async-done | bytes 221216 | tf_op jit(solution)/shard_map/all_to_all | solution.py:153
  105.6 1.5 %fusion.3 = (f32[768]{0:T(1024)S(1)}, f32[768,768]{0,1:T(8,128)S(1)}) fusion(pred[768]{0:T(1024)(128)(4,1)S(1)} %lt.37, bf16[768,72]{1,0:T(8,128)(2,1)} %bitcast.41, bf16[768,144]{1,0:T(8,128)(2,1)S(1)} %bitcast.39), kind=kOutput, calls=%fused_computation.7 | convolution fusion | flops 86703360 | bytes 2670592 | tf_op jit(solution)/shard_map/qhd,khd->hqk/dot_general | solution.py:40
  107.7 0.8 fusion.15
  108.6 0.8 copy.13
  109.4 3.5 %all-to-all-start.2 = ((bf16[16,48,72]{2,1,0:T(8,128)(2,1)}), bf16[16,48,72]{2,1,0:T(8,128)(2,1)S(1)}, u32[]{:S(2)}, u32[]{:S(2)}) async-start(bf16[16,48,72]{2,1,0:T(8,128)(2,1)} %bitcast.10), calls=%async_computation.2 | async-start | bytes 393216 | tf_op jit(solution)/shard_map/all_to_all | solution.py:166
  113.5 0.6 compare_convert_fusion
  114.1 7.7 %all-to-all-done.2 = bf16[16,48,72]{2,1,0:T(8,128)(2,1)S(1)} async-done(((bf16[16,48,72]{2,1,0:T(8,128)(2,1)}), bf16[16,48,72]{2,1,0:T(8,128)(2,1)S(1)}, u32[]{:S(2)}, u32[]{:S(2)}) %all-to-all-start.2) | async-done | bytes 110624 | tf_op jit(solution)/shard_map/all_to_all | solution.py:166
  122.1 1.2 %fusion.2 = bf16[48,1152]{1,0:T(8,128)(2,1)} fusion(bf16[48,1152]{1,0:T(8,128)(2,1)S(1)} %reshape.179, bf16[1152,1152]{1,0:T(8,128)(2,1)S(1)} %copy-done, f32[48]{0:T(128)S(1)} %compare_convert_fusion, f32[1152]{0:T(1024)S(1)} %get-tuple-element.5, f32[48,1152]{1,0:T(8,128)S(1)} %concatenate.13, bf16[48,1152]{1,0:T(8,128)(2,1)S(1)} %copy-done.1), kind=kOutput, calls=%fused_computation.6 | convolution fusion | flops 127733760 | bytes 3211968 | tf_op jit(solution)/shard_map/dot_general | solution.py:171
  (29 shorter events, 3.3 us)
Async XLA Ops:
  0.0 122.1 %copy-start = (bf16[1152,1152]{1,0:T(8,128)(2,1)S(1)}, bf16[1152,1152]{1,0:T(8,128)(2,1)}, u32[]{:S(2)}) copy-start(bf16[1152,1152]{1,0:T(8,128)(2,1)} %param.17) | copy-start | bytes 7962628
  0.0 70.4 %copy-start.1 = (bf16[48,1152]{1,0:T(8,128)(2,1)S(1)}, bf16[48,1152]{1,0:T(8,128)(2,1)}, u32[]{:S(2)}) copy-start(bf16[48,1152]{1,0:T(8,128)(2,1)} %param.9) | copy-start | bytes 331780
  75.0 18.4 %copy-start.3 = (s32[16]{0:T(128)S(1)}, s32[16]{0:T(128)}, u32[]{:S(2)}) copy-start(s32[16]{0:T(128)} %param.11) | copy-start | bytes 196
  76.8 12.5 %all-to-all-start = ((bf16[16,48,72]{2,1,0:T(8,128)(2,1)}), bf16[16,48,72]{2,1,0:T(8,128)(2,1)S(1)}, u32[]{:S(2)}, u32[]{:S(2)}) async-start(bf16[16,48,72]{2,1,0:T(8,128)(2,1)} %bitcast.38), calls=%async_computation | async-start | bytes 393216 | tf_op jit(solution)/shard_map/all_to_all | solution.py:152
  89.2 0.7 copy-start.2
  89.9 15.7 %all-to-all-start.1 = ((bf16[16,48,144]{2,1,0:T(8,128)(2,1)}), bf16[16,48,144]{2,1,0:T(8,128)(2,1)S(1)}, u32[]{:S(2)}, u32[]{:S(2)}) async-start(bf16[16,48,144]{2,1,0:T(8,128)(2,1)} %maximum_bitcast_fusion), calls=%async_computation.1 | async-start | bytes 786432 | tf_op jit(solution)/shard_map/all_to_all | solution.py:153
  109.4 12.5 %all-to-all-start.2 = ((bf16[16,48,72]{2,1,0:T(8,128)(2,1)}), bf16[16,48,72]{2,1,0:T(8,128)(2,1)S(1)}, u32[]{:S(2)}, u32[]{:S(2)}) async-start(bf16[16,48,72]{2,1,0:T(8,128)(2,1)} %bitcast.10), calls=%async_computation.2 | async-start | bytes 393216 | tf_op jit(solution)/shard_map/all_to_all | solution.py:166
where the time goes:
time: 124 us; the launch traced here: 123 us
  blocking collectives  63 us (51%)
  waiting for transfers between devices  24.3 us (20%)
  matrix products  11 us (9%)
  starting transfers between devices  10.6 us (9%)
  other arithmetic  6.94 us (6%)
  local copies, waits for them, and re-layouts  6.71 us (5%)
    psum x1, blocking collectives, per_device(): modulation = lax.psum(partial_mod, 'patch')  63 us
    all_to_all x1, waiting for transfers between devices, per_device(): lax.all_to_all(pair_send, 'patch', split_axis=0, concat_axis=0, tiled=True)  12 us
    all_to_all x1, waiting for transfers between devices, per_device(): lax.all_to_all(head_result, 'patch', split_axis=0, concat_axis=0, tiled=T...  7.68 us
    all_to_all x1, waiting for transfers between devices, per_device(): lax.all_to_all(query_send, 'patch', split_axis=0, concat_axis=0, tiled=True)  4.69 us
    dot_general x1, matrix products, per_device(): jnp.dot(modulated, qkv_weight, preferred_element_type=jnp.float32)  4.6 us
    all_to_all x1, starting transfers between devices, per_device(): lax.all_to_all(pair_send, 'patch', split_axis=0, concat_axis=0, tiled=True)  3.55 us
    all_to_all x1, starting transfers between devices, per_device(): lax.all_to_all(query_send, 'patch', split_axis=0, concat_axis=0, tiled=True)  3.52 us
    all_to_all x1, starting transfers between devices, per_device(): lax.all_to_all(head_result, 'patch', split_axis=0, concat_axis=0, tiled=T...  3.52 us
  transfers between devices with their start and end apart: 3, of which 3 were waited for; matrix products, arithmetic and copies ran while one was open for 5% of the time, Pallas kernels for 0%

commit v1 on v0

--- a/solution.py
+++ b/solution.py
@@ -121,7 +121,7 @@
     cond_part = jnp.dot(hidden_time, time_out, preferred_element_type=jnp.float32)
     activated = jax.nn.silu(cond_part).astype(jnp.bfloat16)
     partial_mod = jnp.dot(activated, ada_weight, preferred_element_type=jnp.float32)
-    modulation = lax.psum(partial_mod, "patch")
+    modulation = jnp.sum(lax.all_gather(partial_mod[0], "patch"), axis=0, keepdims=True)
     shift_mod = modulation[:, :model_width]
     scale_mod = modulation[:, model_width : 2 * model_width]
     gate_mod = modulation[:, 2 * model_width :]

time: 124 us -> 84.9 us (0.68)
  blocking collectives: 63 us -> 23.7 us
    psum x1 -> x0, blocking collectives: 63 us -> none  [per_device(): modulation = lax.psum(partial_mod, 'patch')]
    all_gather x0 -> x1, blocking collectives: none -> 23.7 us  [per_device(): lax.all_gather(partial_mod[0], 'patch')]
  transfers between devices with their start and end apart: 3 -> 3, of which waited for: 3 -> 3; matrix products, arithmetic and copies ran while one was open for 5% -> 7% of each run, Pallas kernels for 0% -> 0%
where the time goes in v1:
time: 84.9 us; the launch traced here: 84.3 us
  waiting for transfers between devices  24.3 us (29%)
  blocking collectives  23.7 us (28%)
  matrix products  11 us (13%)
  starting transfers between devices  10.6 us (12%)
  other arithmetic  7.09 us (8%)
  local copies, waits for them, and re-layouts  6.72 us (8%)
  between operations  0.88 us (1%)
    all_gather x1, blocking collectives, per_device(): lax.all_gather(partial_mod[0], 'patch')  23.7 us
    all_to_all x1, waiting for transfers between devices, per_device(): lax.all_to_all(pair_send, 'patch', split_axis=0, concat_axis=0, tiled=True)  12 us
    all_to_all x1, waiting for transfers between devices, per_device(): lax.all_to_all(head_result, 'patch', split_axis=0, concat_axis=0, tiled=T...  7.68 us
    all_to_all x1, waiting for transfers between devices, per_device(): lax.all_to_all(query_send, 'patch', split_axis=0, concat_axis=0, tiled=True)  4.69 us
    dot_general x1, matrix products, per_device(): jnp.dot(modulated, qkv_weight, preferred_element_type=jnp.float32)  4.61 us
    all_to_all x1, starting transfers between devices, per_device(): lax.all_to_all(pair_send, 'patch', split_axis=0, concat_axis=0, tiled=True)  3.55 us
    all_to_all x1, starting transfers between devices, per_device(): lax.all_to_all(head_result, 'patch', split_axis=0, concat_axis=0, tiled=T...  3.52 us
    all_to_all x1, starting transfers between devices, per_device(): lax.all_to_all(query_send, 'patch', split_axis=0, concat_axis=0, tiled=True)  3.52 us
  transfers between devices with their start and end apart: 3, of which 3 were waited for; matrix products, arithmetic and copies ran while one was open for 7% of the time, Pallas kernels for 0%

profile of v1, /device:TPU:0, one launch (start us, length us, event | category | flops | bytes accessed | tf_op | source)
XLA Modules:
  0.0 84.3 jit_solution(7440912104920625258)
XLA Ops:
  0.0 0.9 %convert_bitcast_fusion = (f32[48]{0:T(128)S(1)}, f32[48]{0:T(128)S(1)}) fusion(s32[2,48]{1,0:T(2,128)} %param.10), kind=kLoop, calls=%fused_computation.55 | loop fusion | flops 96 | bytes 768 | tf_op jit(solution)/shard_map/convert_element_type | solution.py:26
  1.6 1.0 %fusion.25 = f32[48]{0:T(128)S(1)} fusion(f32[48,1152]{1,0:T(8,128)S(1)} %concatenate.13, bf16[48,1152]{1,0:T(8,128)(2,1)} %param.9), kind=kLoop, calls=%fused_computation.34 | loop fusion | flops 165840 | bytes 331968 | tf_op jit(solution)/shard_map/reduce_sum | solution.py:129
  2.7 1.1 %multiply_reduce_fusion = f32[48]{0:T(128)S(1)} fusion(f32[48]{0:T(128)S(1)} %broadcast_multiply_fusion, f32[48,1152]{1,0:T(8,128)S(1)} %concatenate.13, bf16[48,1152]{1,0:T(8,128)(2,1)} %param.9), kind=kLoop, calls=%fused_computation.20 | loop fusion | flops 276432 | bytes 332160 | tf_op jit(solution)/shard_map/reduce_sum | solution.py:131
  4.5 1.3 %convolution_reduce_fusion = f32[1152]{0:T(1024)S(1)} fusion(bf16[256,1]{0,1:T(2,128)(2,1)S(1)} %reshape.184, bf16[256,1152]{1,0:T(8,128)(2,1)} %param.13), kind=kOutput, calls=%fused_computation.16 | convolution fusion | flops 589824 | bytes 594944 | tf_op jit(solution)/shard_map/dot_general | solution.py:119
  5.8 1.6 %convolution_bitcast_fusion = f32[1,1,3456]{2,1,0:T(1,128)S(1)} fusion(bf16[72,3456]{1,0:T(8,128)(2,1)} %param.15, bf16[1152,1]{0,1:T(2,128)(2,1)S(1)} %reshape.186, bf16[1152,72]{0,1:T(8,128)(2,1)} %param.14), kind=kOutput, calls=%fused_computation.1 | convolution fusion | flops 663912 | bytes 679680 | tf_op jit(solution)/shard_map/dot_general | solution.py:123
  7.4 23.7 %all-gather.1 = f32[16,1,3456]{2,1,0:T(1,128)S(1)} all-gather(f32[1,1,3456]{2,1,0:T(1,128)S(1)} %convolution_bitcast_fusion), channel_id=2, replica_groups=mesh['req'=2,'patch'=16] {'patch'}, dimensions={0}, use_global_device_ids=true | all-gather | bytes 235008 | tf_op jit(solution)/shard_map/all_gather | solution.py:124
  31.3 4.6 %convolution_convert_fusion = bf16[48,3456]{1,0:T(8,128)(2,1)S(1)} fusion(bf16[1152,3456]{1,0:T(8,128)(2,1)} %param.16, f32[1152]{0:T(1024)S(1)} %get-tuple-element.6, f32[1152]{0:T(1024)S(1)} %get-tuple-element.7, f32[48]{0:T(128)S(1)} %add_rsqrt_fusion, f32[48]{0:T(128)S(1)} %broadcast_multiply_fusion, f32[48,1152]{1,0:T(8,128)S(1)} %concatenate.13, ...), kind=kOutput, calls=%fused_computation | convolution fusion | flops 382758912 | bytes 8635776 | tf_op jit(solution)/shard_map/dot_general | solution.py:137
  35.9 0.7 fusion.37
  37.0 0.7 copy.21
  37.7 3.5 %all-to-all-start = ((bf16[16,48,72]{2,1,0:T(8,128)(2,1)}), bf16[16,48,72]{2,1,0:T(8,128)(2,1)S(1)}, u32[]{:S(2)}, u32[]{:S(2)}) async-start(bf16[16,48,72]{2,1,0:T(8,128)(2,1)} %bitcast.40), calls=%async_computation | async-start | bytes 393216 | tf_op jit(solution)/shard_map/all_to_all | solution.py:152
  41.2 1.2 %reshape.175 = bf16[48,16,72]{2,1,0:T(8,128)(2,1)S(1)} reshape(bf16[48,1152]{1,0:T(8,128)(2,1)} %get-tuple-element.8) | data formatting | bytes 221184 | tf_op jit(solution)/shard_map/reshape | solution.py:144
  42.5 0.7 copy.16
  43.6 1.8 %maximum_bitcast_fusion = bf16[16,48,144]{2,1,0:T(8,128)(2,1)} fusion(bf16[48,16,72]{2,0,1:T(8,128)(2,1)S(1)} %copy.17, bf16[48,16,72]{2,0,1:T(8,128)(2,1)} %copy.16), kind=kLoop, calls=%fused_computation.18 | loop fusion | flops 442368 | bytes 442368 | tf_op jit(solution)/shard_map/transpose | solution.py:148
  45.4 4.7 %all-to-all-done = bf16[16,48,72]{2,1,0:T(8,128)(2,1)S(1)} async-done(((bf16[16,48,72]{2,1,0:T(8,128)(2,1)}), bf16[16,48,72]{2,1,0:T(8,128)(2,1)S(1)}, u32[]{:S(2)}, u32[]{:S(2)}) %all-to-all-start) | async-done | bytes 110624 | tf_op jit(solution)/shard_map/all_to_all | solution.py:152
  50.1 0.7 copy-done.2
  50.8 3.6 %all-to-all-start.1 = ((bf16[16,48,144]{2,1,0:T(8,128)(2,1)}), bf16[16,48,144]{2,1,0:T(8,128)(2,1)S(1)}, u32[]{:S(2)}, u32[]{:S(2)}) async-start(bf16[16,48,144]{2,1,0:T(8,128)(2,1)} %maximum_bitcast_fusion), calls=%async_computation.1 | async-start | bytes 786432 | tf_op jit(solution)/shard_map/all_to_all | solution.py:153
  54.5 12.0 %all-to-all-done.1 = bf16[16,48,144]{2,1,0:T(8,128)(2,1)S(1)} async-done(((bf16[16,48,144]{2,1,0:T(8,128)(2,1)}), bf16[16,48,144]{2,1,0:T(8,128)(2,1)S(1)}, u32[]{:S(2)}, u32[]{:S(2)}) %all-to-all-start.1) | async-done | bytes 221216 | tf_op jit(solution)/shard_map/all_to_all | solution.py:153
  66.5 1.5 %fusion.3 = (f32[768]{0:T(1024)S(1)}, f32[768,768]{0,1:T(8,128)S(1)}) fusion(pred[768]{0:T(1024)(128)(4,1)S(1)} %lt.37, bf16[768,72]{1,0:T(8,128)(2,1)} %bitcast.43, bf16[768,144]{1,0:T(8,128)(2,1)S(1)} %bitcast.41), kind=kOutput, calls=%fused_computation.8 | convolution fusion | flops 86703360 | bytes 2670592 | tf_op jit(solution)/shard_map/qhd,khd->hqk/dot_general | solution.py:40
  68.6 0.8 fusion.15
  69.5 0.8 copy.18
  70.3 3.5 %all-to-all-start.2 = ((bf16[16,48,72]{2,1,0:T(8,128)(2,1)}), bf16[16,48,72]{2,1,0:T(8,128)(2,1)S(1)}, u32[]{:S(2)}, u32[]{:S(2)}) async-start(bf16[16,48,72]{2,1,0:T(8,128)(2,1)} %bitcast.10), calls=%async_computation.2 | async-start | bytes 393216 | tf_op jit(solution)/shard_map/all_to_all | solution.py:166
  74.4 0.6 compare_convert_fusion
  75.0 7.7 %all-to-all-done.2 = bf16[16,48,72]{2,1,0:T(8,128)(2,1)S(1)} async-done(((bf16[16,48,72]{2,1,0:T(8,128)(2,1)}), bf16[16,48,72]{2,1,0:T(8,128)(2,1)S(1)}, u32[]{:S(2)}, u32[]{:S(2)}) %all-to-all-start.2) | async-done | bytes 110624 | tf_op jit(solution)/shard_map/all_to_all | solution.py:166
  83.0 1.2 %fusion.2 = bf16[48,1152]{1,0:T(8,128)(2,1)} fusion(bf16[48,1152]{1,0:T(8,128)(2,1)S(1)} %reshape.179, bf16[1152,1152]{1,0:T(8,128)(2,1)S(1)} %copy-done, f32[48]{0:T(128)S(1)} %compare_convert_fusion, f32[1152]{0:T(1024)S(1)} %get-tuple-element.5, f32[48,1152]{1,0:T(8,128)S(1)} %concatenate.13, bf16[48,1152]{1,0:T(8,128)(2,1)S(1)} %copy-done.1), kind=kOutput, calls=%fused_computation.7 | convolution fusion | flops 127733760 | bytes 3211968 | tf_op jit(solution)/shard_map/dot_general | solution.py:171
  (31 shorter events, 3.5 us)
Async XLA Ops:
  0.0 83.0 %copy-start = (bf16[1152,1152]{1,0:T(8,128)(2,1)S(1)}, bf16[1152,1152]{1,0:T(8,128)(2,1)}, u32[]{:S(2)}) copy-start(bf16[1152,1152]{1,0:T(8,128)(2,1)} %param.17) | copy-start | bytes 7962628
  0.0 31.3 %copy-start.1 = (bf16[48,1152]{1,0:T(8,128)(2,1)S(1)}, bf16[48,1152]{1,0:T(8,128)(2,1)}, u32[]{:S(2)}) copy-start(bf16[48,1152]{1,0:T(8,128)(2,1)} %param.9) | copy-start | bytes 331780
  35.9 18.4 %copy-start.3 = (s32[16]{0:T(128)S(1)}, s32[16]{0:T(128)}, u32[]{:S(2)}) copy-start(s32[16]{0:T(128)} %param.11) | copy-start | bytes 196
  37.7 12.5 %all-to-all-start = ((bf16[16,48,72]{2,1,0:T(8,128)(2,1)}), bf16[16,48,72]{2,1,0:T(8,128)(2,1)S(1)}, u32[]{:S(2)}, u32[]{:S(2)}) async-start(bf16[16,48,72]{2,1,0:T(8,128)(2,1)} %bitcast.40), calls=%async_computation | async-start | bytes 393216 | tf_op jit(solution)/shard_map/all_to_all | solution.py:152
  50.1 0.7 copy-start.2
  50.8 15.7 %all-to-all-start.1 = ((bf16[16,48,144]{2,1,0:T(8,128)(2,1)}), bf16[16,48,144]{2,1,0:T(8,128)(2,1)S(1)}, u32[]{:S(2)}, u32[]{:S(2)}) async-start(bf16[16,48,144]{2,1,0:T(8,128)(2,1)} %maximum_bitcast_fusion), calls=%async_computation.1 | async-start | bytes 786432 | tf_op jit(solution)/shard_map/all_to_all | solution.py:153
  70.3 12.5 %all-to-all-start.2 = ((bf16[16,48,72]{2,1,0:T(8,128)(2,1)}), bf16[16,48,72]{2,1,0:T(8,128)(2,1)S(1)}, u32[]{:S(2)}, u32[]{:S(2)}) async-start(bf16[16,48,72]{2,1,0:T(8,128)(2,1)} %bitcast.10), calls=%async_computation.2 | async-start | bytes 393216 | tf_op jit(solution)/shard_map/all_to_all | solution.py:166

commit v2 on v1

v2 whole, which is shorter than its diff:
```python
import functools
import math

import jax
import jax.numpy as jnp
import numpy as np
from jax import lax
from jax.experimental import pallas as pl
from jax.experimental.pallas import tpu as pltpu
from jax.sharding import PartitionSpec as P

HEADS = 16
NEG = -1e30
F32 = jnp.float32
BF16 = jnp.bfloat16
MESH = pl.DeviceIdType.MESH


def silu(v):
    return v / (1.0 + jnp.exp(-v))


def dot(a, b):
    return jnp.dot(a, b, preferred_element_type=F32)


def one_row_dot(row, matrix):
    wide = jnp.broadcast_to(row, (16, row.shape[1])).astype(BF16)
    return dot(wide, matrix)[0:1]


def block_kernel(
    n, rows, width, head,
    counts, tstep, pos, pos_tab, time_tab,
    tok_h, tin_h, tout_h, ada_h, qkv_h, ow_h,
    out,
    tok, tin, tout, ada, qkv, ow, mods, xin_s, norm_s, send, got, kbuf, vbuf, att, back,
    lsem, wsem, msend, mrecv, psend, precv, asend, arecv,
):
    me = lax.axis_index("patch")
    my_head = lax.rem(me, HEADS)
    group = me // HEADS
    chunk = HEADS * rows
    groups = n // HEADS
    inv_root = 1.0 / math.sqrt(head)

    barrier = pltpu.get_barrier_semaphore()

    @pl.loop(1, n)
    def _(step):
        pl.semaphore_signal(
            barrier, inc=1, device_id={"patch": lax.rem(me + step, n)}, device_id_type=MESH
        )

    loads = [
        pltpu.make_async_copy(src, dst, lsem.at[i])
        for i, (src, dst) in enumerate(
            [(tin_h, tin), (tout_h, tout), (ada_h, ada), (tok_h, tok), (qkv_h, qkv)]
        )
    ]
    for load in loads:
        load.start()
    ow[:, head:, :] = jnp.zeros((HEADS, ow.shape[1] - head, width), BF16)
    ow_loads = [
        pltpu.make_async_copy(
            ow_h.at[pl.ds(h * head, head), :], ow.at[h, pl.ds(0, head), :], wsem.at[h]
        )
        for h in range(HEADS)
    ]
    for load in ow_loads:
        load.start()

    angles = tstep[0].astype(F32) * time_tab[0:1, :] + time_tab[1:2, :]
    features = jnp.sin(angles).astype(BF16)
    loads[0].wait()
    hidden = silu(one_row_dot(features, tin[...])).astype(BF16)
    loads[1].wait()
    activated = silu(one_row_dot(hidden, tout[...])).astype(BF16)
    loads[2].wait()
    mods[me] = one_row_dot(activated, ada[...])

    pl.semaphore_wait(barrier, n - 1)

    def mod_copy(step, slot):
        return pltpu.make_async_remote_copy(
            src_ref=mods.at[slot],
            dst_ref=mods.at[slot],
            send_sem=msend.at[step],
            recv_sem=mrecv.at[slot],
            device_id={"patch": lax.rem(me + step, n)},
            device_id_type=MESH,
        )

    @pl.loop(1, n)
    def _(step):
        mod_copy(step, me).start()

    ids = lax.broadcasted_iota(jnp.int32, (rows, rows), 0)
    eye = ids == lax.broadcasted_iota(jnp.int32, (rows, rows), 1)
    posf = pos[...].astype(F32)
    row_col = jnp.sum(jnp.where(eye, posf[0:1, :], 0.0), axis=1, keepdims=True)
    col_col = jnp.sum(jnp.where(eye, posf[1:2, :], 0.0), axis=1, keepdims=True)
    lanes = lax.broadcasted_iota(jnp.int32, (1, width), 1)
    first = lanes < width // 2
    place = jnp.where(first, row_col, col_col)
    embed = jnp.sin(place * pos_tab[0:1, :] + pos_tab[1:2, :])
    loads[3].wait()
    x_in = tok[...].astype(F32) + embed
    xin_s[...] = x_in
    centered = x_in - jnp.mean(x_in, axis=1, keepdims=True)
    variance = jnp.mean(centered * centered, axis=1, keepdims=True)
    norm_s[...] = centered * lax.rsqrt(variance + 1e-6)

    @pl.loop(1, n)
    def _(step):
        mod_copy(step, lax.rem(me - step + n, n)).wait_recv()

    modulation = jnp.sum(mods[...], axis=0)
    shift = modulation[:, :width]
    scale = modulation[:, width : 2 * width]
    gate = modulation[:, 2 * width :]
    modulated = (norm_s[...] * (1.0 + scale) + shift).astype(BF16)
    loads[4].wait()
    parts = [
        dot(modulated, qkv[:, i * width : (i + 1) * width]).astype(BF16) for i in range(3)
    ]
    spare = jnp.zeros((rows, send.shape[2] - 3 * head), BF16)
    for h in range(HEADS):
        cols = slice(h * head, (h + 1) * head)
        send[h] = jnp.concatenate([part[:, cols] for part in parts] + [spare], axis=1)

    def pair_copy(step, slot):
        to = lax.rem(me + step, n)
        return pltpu.make_async_remote_copy(
            src_ref=send.at[lax.rem(to, HEADS)],
            dst_ref=got.at[slot],
            send_sem=psend.at[step],
            recv_sem=precv.at[slot],
            device_id={"patch": to},
            device_id_type=MESH,
        )

    @pl.loop(1, n)
    def _(step):
        pair_copy(step, me).start()

    got[me] = send[my_head]
    vbuf[...] = jnp.zeros(vbuf.shape, BF16)

    @pl.loop(1, n)
    def _(step):
        pair_copy(step, lax.rem(me - step + n, n)).wait_recv()

    for g in range(groups):
        block = got[g * HEADS : (g + 1) * HEADS].reshape(chunk, got.shape[2])
        kbuf[g * chunk : (g + 1) * chunk, :] = block[:, head : 2 * head]
        vbuf[g * chunk : (g + 1) * chunk, :head] = block[:, 2 * head : 3 * head]

    def mask_of(g):
        slots = lax.broadcasted_iota(jnp.int32, (1, chunk), 1)
        bias = jnp.full((1, chunk), NEG, F32)
        for b in range(HEADS):
            inside = (slots >= b * rows) & (slots < b * rows + counts[g * HEADS + b])
            bias = jnp.where(inside, 0.0, bias)
        return bias

    masks = [mask_of(g) for g in range(groups)]

    def att_copy(j, slot, to):
        return pltpu.make_async_remote_copy(
            src_ref=att.at[j],
            dst_ref=back.at[slot],
            send_sem=asend.at[j],
            recv_sem=arecv.at[slot],
            device_id={"patch": group * HEADS + to},
            device_id_type=MESH,
        )

    pairs = 2

    @pl.loop(0, HEADS // pairs)
    def _(step):
        base = lax.rem(my_head // pairs + 1 + step, HEADS // pairs) * pairs
        block = got[pl.ds(group * HEADS + base, pairs)].reshape(pairs * rows, got.shape[2])
        query = block[:, :head]
        top = total = weighted = None
        for g in range(groups):
            keys = kbuf[g * chunk : (g + 1) * chunk, :]
            scores = lax.dot_general(
                query, keys, (((1,), (1,)), ((), ())), preferred_element_type=F32
            )
            scores = scores * inv_root + masks[g]
            new_top = jnp.max(scores, axis=1, keepdims=True)
            if g:
                new_top = jnp.maximum(top, new_top)
            prob = jnp.exp(scores - new_top)
            mass = jnp.sum(prob, axis=1, keepdims=True)
            mixed = dot(prob.astype(BF16), vbuf[g * chunk : (g + 1) * chunk, :])
            if g:
                factor = jnp.exp(top - new_top)
                mass = total * factor + mass
                mixed = weighted * factor + mixed
            top, total, weighted = new_top, mass, mixed
        att[pl.ds(base, pairs)] = (
            (weighted / total).astype(BF16).reshape(pairs, rows, att.shape[2])
        )
        for i in range(pairs):

            @pl.when(base + i != my_head)
            def _():
                att_copy(base + i, my_head, base + i).start()

    back[my_head] = att[my_head]
    for load in ow_loads:
        load.wait()

    @pl.loop(1, HEADS)
    def _(step):
        other = lax.rem(my_head + step, HEADS)
        att_copy(other, other, other).wait_recv()

    attended = jnp.concatenate([back[h] for h in range(HEADS)], axis=1)
    projected = dot(attended, ow[...].reshape(HEADS * ow.shape[1], width))
    valid = (lax.broadcasted_iota(jnp.int32, (rows, 1), 0) < counts[me]).astype(F32)
    out[...] = (xin_s[...] + gate * projected * valid).astype(BF16)

    @pl.loop(1, n)
    def _(step):
        mod_copy(step, me).wait_send()
        pair_copy(step, me).wait_send()

    @pl.loop(1, HEADS)
    def _(step):
        other = lax.rem(my_head + step, HEADS)
        att_copy(other, other, other).wait_send()


def tables(width, freq):
    quarter, half = width // 4, freq // 2
    omega = np.power(10000.0, -np.arange(quarter) / quarter)
    turn = math.pi / 2
    pos_tab = np.stack([np.tile(omega, 4), np.repeat([0.0, turn, 0.0, turn], quarter)])
    wave = np.exp(-math.log(10000.0) * np.arange(half) / half)
    time_tab = np.stack([np.tile(wave, 2), np.repeat([turn, 0.0], half)])
    return pos_tab.astype(np.float32), time_tab.astype(np.float32)


def per_device(
    tokens, positions, counts, timestep, time_in, time_out, ada_weight, qkv_weight, out_weight
):
    n = lax.axis_size("patch")
    rows, width = tokens.shape
    head = width // HEADS
    lane = 128
    head_pad = -(-head // lane) * lane
    pack = -(-3 * head // lane) * lane
    pos_tab, time_tab = tables(width, time_in.shape[0])
    smem = pl.BlockSpec(memory_space=pltpu.SMEM)
    vmem = pl.BlockSpec(memory_space=pltpu.VMEM)
    hbm = pl.BlockSpec(memory_space=pl.ANY)
    return pl.pallas_call(
        functools.partial(block_kernel, n, rows, width, head),
        out_shape=jax.ShapeDtypeStruct((rows, width), BF16),
        in_specs=[smem, smem, vmem, vmem, vmem] + [hbm] * 6,
        out_specs=vmem,
        scratch_shapes=[
            pltpu.VMEM(tokens.shape, BF16),
            pltpu.VMEM(time_in.shape, BF16),
            pltpu.VMEM(time_out.shape, BF16),
            pltpu.VMEM(ada_weight.shape, BF16),
            pltpu.VMEM(qkv_weight.shape, BF16),
            pltpu.VMEM((HEADS, head_pad, width), BF16),
            pltpu.VMEM((n, 1, 3 * width), F32),
            pltpu.VMEM((rows, width), F32),
            pltpu.VMEM((rows, width), F32),
            pltpu.VMEM((HEADS, rows, pack), BF16),
            pltpu.VMEM((n, rows, pack), BF16),
            pltpu.VMEM((n * rows, head), BF16),
            pltpu.VMEM((n * rows, head_pad), BF16),
            pltpu.VMEM((HEADS, rows, head_pad), BF16),
            pltpu.VMEM((HEADS, rows, head_pad), BF16),
            pltpu.SemaphoreType.DMA((5,)),
            pltpu.SemaphoreType.DMA((HEADS,)),
            pltpu.SemaphoreType.DMA((n,)),
            pltpu.SemaphoreType.DMA((n,)),
            pltpu.SemaphoreType.DMA((n,)),
            pltpu.SemaphoreType.DMA((n,)),
            pltpu.SemaphoreType.DMA((HEADS,)),
            pltpu.SemaphoreType.DMA((HEADS,)),
        ],
        compiler_params=pltpu.CompilerParams(
            collective_id=0, has_side_effects=True, vmem_limit_bytes=60 * 2**20
        ),
    )(
        counts, timestep, positions, pos_tab, time_tab,
        tokens, time_in, time_out, ada_weight, qkv_weight, out_weight,
    )


def solution(mesh):
    placed = (
        P(("req", "patch"), None),
        P(None, ("req", "patch")),
        P("req"),
        P("req"),
        P(),
        P(None, "patch"),
        P("patch", None),
        P(),
        P(),
    )
    return jax.shard_map(
        per_device, mesh=mesh, in_specs=placed, out_specs=P(("req", "patch"), None), check_vma=False
    )
```

time: 84.9 us -> 38.5 us (0.45)
  Pallas kernels: 0 us -> 34.3 us
  waiting for transfers between devices: 24.3 us -> 0 us
  blocking collectives: 23.7 us -> 0 us
  matrix products: 11 us -> 0 us
  starting transfers between devices: 10.6 us -> 0 us
  other arithmetic: 7.09 us -> 0 us
  local copies, waits for them, and re-layouts: 6.72 us -> 3.35 us
    pallas_call x0 -> x1, Pallas kernels: none -> 34.3 us  [per_device(): pl.pallas_call(functools.partial(block_kernel, n, rows, width, head), out...]
    all_to_all x3 -> x0, waiting for transfers between devices: 24.3 us -> none  [the longest x1 12 us: per_device(): lax.all_to_all(pair_send, 'patch', split_axis=0, concat_axis=0, tiled=True)]
    all_gather x1 -> x0, blocking collectives: 23.7 us -> none  [per_device(): lax.all_gather(partial_mod[0], 'patch')]
    dot_general x6 -> x0, matrix products: 11 us -> none  [the longest x1 4.61 us: per_device(): jnp.dot(modulated, qkv_weight, preferred_element_type=jnp.float32)]
    all_to_all x3 -> x0, starting transfers between devices: 10.6 us -> none  [the longest x1 3.55 us: per_device(): lax.all_to_all(pair_send, 'patch', split_axis=0, concat_axis=0, tiled=True)]
    reshape x7 -> x0, local copies, waits for them, and re-layouts: 3.66 us -> none  [the longest x2 1.97 us: per_device(): projections[:, model_width:2 * model_width]]
    reduce_sum x4 -> x0, other arithmetic: 2.9 us -> none  [the longest x1 1.1 us: per_device(): variance = jnp.mean(centered * centered, axis=1, keepdims=True)]
    unnamed x8 -> x2, local copies, waits for them, and re-layouts: 0.68 us -> 3.35 us
  transfers between devices with their start and end apart: 3 -> 0, of which waited for: 3 -> 0; matrix products, arithmetic and copies ran while one was open for 7% -> 0% of each run, Pallas kernels for 0% -> 0%
where the time goes in v2:
time: 38.5 us; the launch traced here: 38.3 us
  Pallas kernels  34.3 us (89%)
  local copies, waits for them, and re-layouts  3.35 us (9%)
  between operations  0.66 us (2%)
    pallas_call x1, Pallas kernels, per_device(): pl.pallas_call(functools.partial(block_kernel, n, rows, width, head), out...  34.3 us
    unnamed x2, local copies, waits for them, and re-layouts  3.35 us

profile of v2, /device:TPU:0, one launch (start us, length us, event | category | flops | bytes accessed | tf_op | source)
XLA Modules:
  0.0 38.3 jit_solution(4315148360224701431)
XLA Ops:
  0.7 1.8 %copy.12.tout_h = bf16[1152,72]{1,0:T(8,128)(2,1)} copy(bf16[1152,72]{0,1:T(8,128)(2,1)} %param.16) | data formatting | bytes 331776 | tf_op args[5]
  2.5 34.3 %shard_map.109 = bf16[48,1152]{1,0:T(8,128)(2,1)} custom-call(s32[16]{0:T(128)} %counts.1, s32[1]{0:T(128)S(6)} %copy.14.tstep, s32[2,48]{1,0:T(2,128)} %pos.1, f32[2,1152]{1,0:T(2,128)} %constant.4.clone.pos_tab, f32[2,256]{1,0:T(2,128)} %constant.5.clone.time_tab, bf16[48,1152]{1,0:T(8,128)(2,1)} %tok_h.1, bf16[256,1152]{1,0:T(8,128)(2,1)} %tin_h.1, ...), custom_call_target="tpu_custom_call" | custom-call | tf_op jit(solution)/shard_map/pallas_call | solution.py:261
  36.7 1.6 %copy.15 = bf16[48,1152]{1,0:T(8,128)(2,1)} copy(bf16[48,1152]{1,0:T(8,128)(2,1)} %shard_map.109) | data formatting | bytes 221184

commit v3 on v2

--- a/solution.py
+++ b/solution.py
@@ -34,15 +34,15 @@
     counts, tstep, pos, pos_tab, time_tab,
     tok_h, tin_h, tout_h, ada_h, qkv_h, ow_h,
     out,
-    tok, tin, tout, ada, qkv, ow, mods, xin_s, norm_s, send, got, kbuf, vbuf, att, back,
-    lsem, wsem, msend, mrecv, psend, precv, asend, arecv,
+    tok, tin, tout, ada, qkv, ow, mods, gates, xin_s, norm_s, send, got, kbuf, vbuf, att, back,
+    lsem, wsem, msend, mrecv, gsend, grecv, psend, precv, asend, arecv,
 ):
     me = lax.axis_index("patch")
     my_head = lax.rem(me, HEADS)
     group = me // HEADS
     chunk = HEADS * rows
     groups = n // HEADS
-    inv_root = 1.0 / math.sqrt(head)
+    inv_root = math.log2(math.e) / math.sqrt(head)
 
     barrier = pltpu.get_barrier_semaphore()
 
@@ -75,9 +75,15 @@
     loads[0].wait()
     hidden = silu(one_row_dot(features, tin[...])).astype(BF16)
     loads[1].wait()
-    activated = silu(one_row_dot(hidden, tout[...])).astype(BF16)
+    wide = jnp.broadcast_to(hidden, (16, width))
+    cond = lax.dot_general(wide, tout[...], (((1,), (1,)), ((), ())), preferred_element_type=F32)
+    activated = silu(cond[0:1]).astype(BF16)
     loads[2].wait()
-    mods[me] = one_row_dot(activated, ada[...])
+    partial = one_row_dot(activated, ada[...])
+    mods[me] = jnp.concatenate(
+        [partial[:, :width], partial[:, width : 2 * width]], axis=0
+    ).astype(BF16)
+    gates[me] = partial[:, 2 * width :]
 
     pl.semaphore_wait(barrier, n - 1)
 
@@ -87,6 +93,16 @@
             dst_ref=mods.at[slot],
             send_sem=msend.at[step],
             recv_sem=mrecv.at[slot],
+            device_id={"patch": lax.rem(me + step, n)},
+            device_id_type=MESH,
+        )
+
+    def gate_copy(step, slot):
+        return pltpu.make_async_remote_copy(
+            src_ref=gates.at[slot],
+            dst_ref=gates.at[slot],
+            send_sem=gsend.at[step],
+            recv_sem=grecv.at[slot],
             device_id={"patch": lax.rem(me + step, n)},
             device_id_type=MESH,
         )
@@ -115,10 +131,9 @@
     def _(step):
         mod_copy(step, lax.rem(me - step + n, n)).wait_recv()
 
-    modulation = jnp.sum(mods[...], axis=0)
-    shift = modulation[:, :width]
-    scale = modulation[:, width : 2 * width]
-    gate = modulation[:, 2 * width :]
+    modulation = jnp.sum(mods[...].astype(F32), axis=0)
+    shift = modulation[0:1]
+    scale = modulation[1:2]
     modulated = (norm_s[...] * (1.0 + scale) + shift).astype(BF16)
     loads[4].wait()
     parts = [
@@ -145,26 +160,30 @@
         pair_copy(step, me).start()
 
     got[me] = send[my_head]
-    vbuf[...] = jnp.zeros(vbuf.shape, BF16)
+    tail = lax.broadcasted_iota(jnp.int32, (chunk, vbuf.shape[1] - head), 1)
+    ones = jnp.where(tail == 0, 1.0, 0.0).astype(BF16)
+    slot_ids = lax.broadcasted_iota(jnp.int32, (rows, 1), 0)
+    lane_ids = lax.broadcasted_iota(jnp.int32, (rows, kbuf.shape[1]), 1)
+    for g in range(groups):
+        vbuf[g * chunk : (g + 1) * chunk, head:] = ones
+    for b in range(n):
+        bias = jnp.where(slot_ids < counts[b], 0.0, NEG)
+        kbuf[b * rows : (b + 1) * rows, :] = jnp.where(lane_ids == head, bias, 0.0).astype(BF16)
 
     @pl.loop(1, n)
     def _(step):
         pair_copy(step, lax.rem(me - step + n, n)).wait_recv()
+
+    @pl.loop(1, n)
+    def _(step):
+        gate_copy(step, me).start()
+
 
     for g in range(groups):
         block = got[g * HEADS : (g + 1) * HEADS].reshape(chunk, got.shape[2])
-        kbuf[g * chunk : (g + 1) * chunk, :] = block[:, head : 2 * head]
+        kbuf[g * chunk : (g + 1) * chunk, :head] = block[:, head : 2 * head]
         vbuf[g * chunk : (g + 1) * chunk, :head] = block[:, 2 * head : 3 * head]
 
-    def mask_of(g):
-        slots = lax.broadcasted_iota(jnp.int32, (1, chunk), 1)
-        bias = jnp.full((1, chunk), NEG, F32)
-        for b in range(HEADS):
-            inside = (slots >= b * rows) & (slots < b * rows + counts[g * HEADS + b])
-            bias = jnp.where(inside, 0.0, bias)
-        return bias
-
-    masks = [mask_of(g) for g in range(groups)]
 
     def att_copy(j, slot, to):
         return pltpu.make_async_remote_copy(
@@ -182,25 +201,27 @@
     def _(step):
         base = lax.rem(my_head // pairs + 1 + step, HEADS // pairs) * pairs
         block = got[pl.ds(group * HEADS + base, pairs)].reshape(pairs * rows, got.shape[2])
-        query = block[:, :head]
-        top = total = weighted = None
+        query = jnp.concatenate(
+            [block[:, :head], jnp.ones((pairs * rows, 1), BF16)], axis=1
+        )
+        query = jnp.concatenate(
+            [query, jnp.zeros((pairs * rows, kbuf.shape[1] - head - 1), BF16)], axis=1
+        )
+        top = weighted = None
         for g in range(groups):
             keys = kbuf[g * chunk : (g + 1) * chunk, :]
             scores = lax.dot_general(
                 query, keys, (((1,), (1,)), ((), ())), preferred_element_type=F32
             )
-            scores = scores * inv_root + masks[g]
             new_top = jnp.max(scores, axis=1, keepdims=True)
             if g:
                 new_top = jnp.maximum(top, new_top)
-            prob = jnp.exp(scores - new_top)
-            mass = jnp.sum(prob, axis=1, keepdims=True)
-            mixed = dot(prob.astype(BF16), vbuf[g * chunk : (g + 1) * chunk, :])
+            prob = jnp.exp2((scores - new_top) * inv_root).astype(BF16)
+            mixed = dot(prob, vbuf[g * chunk : (g + 1) * chunk, :])
             if g:
-                factor = jnp.exp(top - new_top)
-                mass = total * factor + mass
-                mixed = weighted * factor + mixed
-            top, total, weighted = new_top, mass, mixed
+                mixed = weighted * jnp.exp2((top - new_top) * inv_root) + mixed
+            top, weighted = new_top, mixed
+        total = weighted[:, head : head + 1]
         att[pl.ds(base, pairs)] = (
             (weighted / total).astype(BF16).reshape(pairs, rows, att.shape[2])
         )
@@ -219,15 +240,21 @@
         other = lax.rem(my_head + step, HEADS)
         att_copy(other, other, other).wait_recv()
 
+    @pl.loop(1, n)
+    def _(step):
+        gate_copy(step, lax.rem(me - step + n, n)).wait_recv()
+
+    gate = jnp.sum(gates[...], axis=0)
     attended = jnp.concatenate([back[h] for h in range(HEADS)], axis=1)
     projected = dot(attended, ow[...].reshape(HEADS * ow.shape[1], width))
     valid = (lax.broadcasted_iota(jnp.int32, (rows, 1), 0) < counts[me]).astype(F32)
-    out[...] = (xin_s[...] + gate * projected * valid).astype(BF16)
+    out[...] = xin_s[...] + gate * projected * valid
 
     @pl.loop(1, n)
     def _(step):
         mod_copy(step, me).wait_send()
         pair_copy(step, me).wait_send()
+        gate_copy(step, me).wait_send()
 
     @pl.loop(1, HEADS)
     def _(step):
@@ -258,29 +285,32 @@
     smem = pl.BlockSpec(memory_space=pltpu.SMEM)
     vmem = pl.BlockSpec(memory_space=pltpu.VMEM)
     hbm = pl.BlockSpec(memory_space=pl.ANY)
-    return pl.pallas_call(
+    result = pl.pallas_call(
         functools.partial(block_kernel, n, rows, width, head),
-        out_shape=jax.ShapeDtypeStruct((rows, width), BF16),
+        out_shape=jax.ShapeDtypeStruct((rows, width), F32),
         in_specs=[smem, smem, vmem, vmem, vmem] + [hbm] * 6,
         out_specs=vmem,
         scratch_shapes=[
             pltpu.VMEM(tokens.shape, BF16),
             pltpu.VMEM(time_in.shape, BF16),
-            pltpu.VMEM(time_out.shape, BF16),
+            pltpu.VMEM(time_out.shape[::-1], BF16),
             pltpu.VMEM(ada_weight.shape, BF16),
             pltpu.VMEM(qkv_weight.shape, BF16),
             pltpu.VMEM((HEADS, head_pad, width), BF16),
-            pltpu.VMEM((n, 1, 3 * width), F32),
+            pltpu.VMEM((n, 2, width), BF16),
+            pltpu.VMEM((n, 1, width), F32),
             pltpu.VMEM((rows, width), F32),
             pltpu.VMEM((rows, width), F32),
             pltpu.VMEM((HEADS, rows, pack), BF16),
             pltpu.VMEM((n, rows, pack), BF16),
-            pltpu.VMEM((n * rows, head), BF16),
+            pltpu.VMEM((n * rows, head_pad), BF16),
             pltpu.VMEM((n * rows, head_pad), BF16),
             pltpu.VMEM((HEADS, rows, head_pad), BF16),
             pltpu.VMEM((HEADS, rows, head_pad), BF16),
             pltpu.SemaphoreType.DMA((5,)),
             pltpu.SemaphoreType.DMA((HEADS,)),
+            pltpu.SemaphoreType.DMA((n,)),
+            pltpu.SemaphoreType.DMA((n,)),
             pltpu.SemaphoreType.DMA((n,)),
             pltpu.SemaphoreType.DMA((n,)),
             pltpu.SemaphoreType.DMA((n,)),
@@ -293,8 +323,9 @@
         ),
     )(
         counts, timestep, positions, pos_tab, time_tab,
-        tokens, time_in, time_out, ada_weight, qkv_weight, out_weight,
+        tokens, time_in, time_out.T, ada_weight, qkv_weight, out_weight,
     )
+    return result.astype(BF16)
 
 
 def solution(mesh):

time: 38.5 us -> 35.4 us (0.919)
  local copies, waits for them, and re-layouts: 3.35 us -> 0 us
  other arithmetic: 0 us -> 1.59 us
  Pallas kernels: 34.3 us -> 33 us
    unnamed x2 -> x0, local copies, waits for them, and re-layouts: 3.35 us -> none
    convert_element_type x0 -> x1, other arithmetic: none -> 1.59 us  [per_device(): return result.astype(BF16)]
    pallas_call x1, Pallas kernels: 34.3 us -> 33 us  [per_device(): pl.pallas_call(functools.partial(block_kernel, n, rows, width, head), out...]
where the time goes in v3:
time: 35.4 us; the launch traced here: 35.2 us
  Pallas kernels  33 us (93%)
  other arithmetic  1.59 us (4%)
  between operations  0.66 us (2%)
    pallas_call x1, Pallas kernels, per_device(): pl.pallas_call(functools.partial(block_kernel, n, rows, width, head), out...  33 us
    convert_element_type x1, other arithmetic, per_device(): return result.astype(BF16)  1.59 us

profile of v3, /device:TPU:0, one launch (start us, length us, event | category | flops | bytes accessed | tf_op | source)
XLA Modules:
  0.0 35.2 jit_solution(7655990881540187764)
XLA Ops:
  0.7 33.0 %shard_map.109 = f32[48,1152]{1,0:T(8,128)} custom-call(s32[16]{0:T(128)} %counts.1, s32[1]{0:T(128)S(6)} %copy.12.tstep, s32[2,48]{1,0:T(2,128)} %pos.1, f32[2,1152]{1,0:T(2,128)} %constant.4.clone.pos_tab, f32[2,256]{1,0:T(2,128)} %constant.5.clone.time_tab, bf16[48,1152]{1,0:T(8,128)(2,1)} %tok_h.1, bf16[256,1152]{1,0:T(8,128)(2,1)} %tin_h.1, ...), custom_call_target="tpu_custom_call" | custom-call | tf_op jit(solution)/shard_map/pallas_call | solution.py:288
  33.6 1.6 %convert_element_type.3 = bf16[48,1152]{1,0:T(8,128)(2,1)} convert(f32[48,1152]{1,0:T(8,128)} %shard_map.109) | non-fusion elementwise | flops 55296 | bytes 331776 | tf_op jit(solution)/shard_map/convert_element_type | solution.py:328

commit v4 on v3

--- a/solution.py
+++ b/solution.py
@@ -27,6 +27,33 @@
 def one_row_dot(row, matrix):
     wide = jnp.broadcast_to(row, (16, row.shape[1])).astype(BF16)
     return dot(wide, matrix)[0:1]
+
+
+def fold_group(rows, extra):
+    group = 8
+    while rows // group * extra > 128:
+        group *= 2
+    return group
+
+
+def fold(block):
+    rows, extra = block.shape[0], block.shape[1] - 64
+    group = fold_group(rows, extra)
+    half = rows // 2
+    main = jnp.concatenate([block[:half, :64], block[half:, :64]], axis=1)
+    pieces = [block[r : r + group, 64:] for r in range(0, rows, group)]
+    spare = 128 - extra * len(pieces)
+    rest = jnp.concatenate(pieces + [jnp.zeros((group, spare), F32)], axis=1)
+    return jnp.concatenate([main, rest], axis=0)
+
+
+def unfold(packed, rows, extra):
+    half = rows // 2
+    left = jnp.concatenate([packed[:half, :64], packed[:half, 64:]], axis=0)
+    rest = packed[half:]
+    count = rows // fold_group(rows, extra)
+    right = jnp.concatenate([rest[:, r * extra : (r + 1) * extra] for r in range(count)], axis=0)
+    return jnp.concatenate([left, right], axis=1)
 
 
 def block_kernel(
@@ -58,16 +85,7 @@
             [(tin_h, tin), (tout_h, tout), (ada_h, ada), (tok_h, tok), (qkv_h, qkv)]
         )
     ]
-    for load in loads:
-        load.start()
-    ow[:, head:, :] = jnp.zeros((HEADS, ow.shape[1] - head, width), BF16)
-    ow_loads = [
-        pltpu.make_async_copy(
-            ow_h.at[pl.ds(h * head, head), :], ow.at[h, pl.ds(0, head), :], wsem.at[h]
-        )
-        for h in range(HEADS)
-    ]
-    for load in ow_loads:
+    for load in loads[:3]:
         load.start()
 
     angles = tstep[0].astype(F32) * time_tab[0:1, :] + time_tab[1:2, :]
@@ -83,7 +101,12 @@
     mods[me] = jnp.concatenate(
         [partial[:, :width], partial[:, width : 2 * width]], axis=0
     ).astype(BF16)
-    gates[me] = partial[:, 2 * width :]
+    span = gates.shape[2]
+    gates[me] = jnp.concatenate(
+        [partial[:, 2 * width : 2 * width + span], partial[:, 3 * width - span :]], axis=0
+    ).astype(BF16)
+    for load in loads[3:]:
+        load.start()
 
     pl.semaphore_wait(barrier, n - 1)
 
@@ -110,6 +133,16 @@
     @pl.loop(1, n)
     def _(step):
         mod_copy(step, me).start()
+
+    ow[:, head:, :] = jnp.zeros((HEADS, ow.shape[1] - head, width), BF16)
+    ow_loads = [
+        pltpu.make_async_copy(
+            ow_h.at[pl.ds(h * head, head), :], ow.at[h, pl.ds(0, head), :], wsem.at[h]
+        )
+        for h in range(HEADS)
+    ]
+    for load in ow_loads:
+        load.start()
 
     ids = lax.broadcasted_iota(jnp.int32, (rows, rows), 0)
     eye = ids == lax.broadcasted_iota(jnp.int32, (rows, rows), 1)
@@ -131,33 +164,60 @@
     def _(step):
         mod_copy(step, lax.rem(me - step + n, n)).wait_recv()
 
+    @pl.loop(1, n)
+    def _(step):
+        gate_copy(step, me).start()
+
     modulation = jnp.sum(mods[...].astype(F32), axis=0)
     shift = modulation[0:1]
     scale = modulation[1:2]
     modulated = (norm_s[...] * (1.0 + scale) + shift).astype(BF16)
     loads[4].wait()
-    parts = [
-        dot(modulated, qkv[:, i * width : (i + 1) * width]).astype(BF16) for i in range(3)
-    ]
     spare = jnp.zeros((rows, send.shape[2] - 3 * head), BF16)
-    for h in range(HEADS):
-        cols = slice(h * head, (h + 1) * head)
-        send[h] = jnp.concatenate([part[:, cols] for part in parts] + [spare], axis=1)
-
-    def pair_copy(step, slot):
-        to = lax.rem(me + step, n)
+    part_heads = HEADS // 2
+
+    def pair_copy(to, slot):
         return pltpu.make_async_remote_copy(
             src_ref=send.at[lax.rem(to, HEADS)],
             dst_ref=got.at[slot],
-            send_sem=psend.at[step],
+            send_sem=psend.at[to],
             recv_sem=precv.at[slot],
             device_id={"patch": to},
             device_id_type=MESH,
         )
 
-    @pl.loop(1, n)
-    def _(step):
-        pair_copy(step, me).start()
+    def make_half(half):
+        low = half * part_heads * head
+        start = low // 128 * 128
+        stop = -(-(low + part_heads * head) // 128) * 128
+        parts = [
+            dot(modulated, qkv[:, i * width + start : i * width + stop]).astype(BF16)
+            for i in range(3)
+        ]
+        for h in range(part_heads):
+            cols = slice(low - start + h * head, low - start + (h + 1) * head)
+            send[half * part_heads + h] = jnp.concatenate(
+                [part[:, cols] for part in parts] + [spare], axis=1
+            )
+
+        @pl.loop(0, groups * part_heads)
+        def _(j):
+            turn = lax.rem(me + j, part_heads)
+            to = (j // part_heads) * HEADS + half * part_heads + turn
+
+            @pl.when(to != me)
+            def _():
+                pair_copy(to, me).start()
+
+    @pl.when(my_head < part_heads)
+    def _():
+        make_half(1)
+        make_half(0)
+
+    @pl.when(my_head >= part_heads)
+    def _():
+        make_half(0)
+        make_half(1)
 
     got[me] = send[my_head]
     tail = lax.broadcasted_iota(jnp.int32, (chunk, vbuf.shape[1] - head), 1)
@@ -172,12 +232,7 @@
 
     @pl.loop(1, n)
     def _(step):
-        pair_copy(step, lax.rem(me - step + n, n)).wait_recv()
-
-    @pl.loop(1, n)
-    def _(step):
-        gate_copy(step, me).start()
-
+        pair_copy(me, lax.rem(me - step + n, n)).wait_recv()
 
     for g in range(groups):
         block = got[g * HEADS : (g + 1) * HEADS].reshape(chunk, got.shape[2])
@@ -195,11 +250,13 @@
             device_id_type=MESH,
         )
 
-    pairs = 2
+    pairs = HEADS // 4
+    mine = my_head // pairs
 
     @pl.loop(0, HEADS // pairs)
     def _(step):
-        base = lax.rem(my_head // pairs + 1 + step, HEADS // pairs) * pairs
+        base = lax.rem(mine // 2 + 1 + step // 2, 2) * 2 + lax.rem(mine + 1 + step, 2)
+        base = base * pairs
         block = got[pl.ds(group * HEADS + base, pairs)].reshape(pairs * rows, got.shape[2])
         query = jnp.concatenate(
             [block[:, :head], jnp.ones((pairs * rows, 1), BF16)], axis=1
@@ -222,9 +279,9 @@
                 mixed = weighted * jnp.exp2((top - new_top) * inv_root) + mixed
             top, weighted = new_top, mixed
         total = weighted[:, head : head + 1]
-        att[pl.ds(base, pairs)] = (
-            (weighted / total).astype(BF16).reshape(pairs, rows, att.shape[2])
-        )
+        result = weighted / total
+        for i in range(pairs):
+            att[base + i] = fold(result[i * rows : (i + 1) * rows, :head]).astype(BF16)
         for i in range(pairs):
 
             @pl.when(base + i != my_head)
@@ -232,29 +289,39 @@
                 att_copy(base + i, my_head, base + i).start()
 
     back[my_head] = att[my_head]
+    filler = jnp.zeros((rows, ow.shape[1] - head), F32)
     for load in ow_loads:
         load.wait()
 
+    @pl.loop(1, n)
+    def _(step):
+        gate_copy(step, lax.rem(me - step + n, n)).wait_recv()
+
+    gate_rows = jnp.sum(gates[...].astype(F32), axis=0)
+    gate = jnp.concatenate([gate_rows[0:1], gate_rows[1:2, 2 * span - width :]], axis=1)
+
+    @pl.loop(1, n)
+    def _(step):
+        mod_copy(step, me).wait_send()
+        pair_copy(lax.rem(me + step, n), me).wait_send()
+        gate_copy(step, me).wait_send()
+
     @pl.loop(1, HEADS)
     def _(step):
         other = lax.rem(my_head + step, HEADS)
         att_copy(other, other, other).wait_recv()
 
-    @pl.loop(1, n)
-    def _(step):
-        gate_copy(step, lax.rem(me - step + n, n)).wait_recv()
-
-    gate = jnp.sum(gates[...], axis=0)
-    attended = jnp.concatenate([back[h] for h in range(HEADS)], axis=1)
+    attended = jnp.concatenate(
+        [
+            piece
+            for h in range(HEADS)
+            for piece in (unfold(back[h].astype(F32), rows, head - 64), filler)
+        ],
+        axis=1,
+    ).astype(BF16)
     projected = dot(attended, ow[...].reshape(HEADS * ow.shape[1], width))
     valid = (lax.broadcasted_iota(jnp.int32, (rows, 1), 0) < counts[me]).astype(F32)
-    out[...] = xin_s[...] + gate * projected * valid
-
-    @pl.loop(1, n)
-    def _(step):
-        mod_copy(step, me).wait_send()
-        pair_copy(step, me).wait_send()
-        gate_copy(step, me).wait_send()
+    out[...] = (xin_s[...] + gate * projected * valid).astype(BF16)
 
     @pl.loop(1, HEADS)
     def _(step):
@@ -281,13 +348,14 @@
     lane = 128
     head_pad = -(-head // lane) * lane
     pack = -(-3 * head // lane) * lane
+    fold_back = rows // 2 + fold_group(rows, head - 64)
     pos_tab, time_tab = tables(width, time_in.shape[0])
     smem = pl.BlockSpec(memory_space=pltpu.SMEM)
     vmem = pl.BlockSpec(memory_space=pltpu.VMEM)
     hbm = pl.BlockSpec(memory_space=pl.ANY)
     result = pl.pallas_call(
         functools.partial(block_kernel, n, rows, width, head),
-        out_shape=jax.ShapeDtypeStruct((rows, width), F32),
+        out_shape=jax.ShapeDtypeStruct((rows, width), BF16),
         in_specs=[smem, smem, vmem, vmem, vmem] + [hbm] * 6,
         out_specs=vmem,
         scratch_shapes=[
@@ -298,15 +366,15 @@
             pltpu.VMEM(qkv_weight.shape, BF16),
             pltpu.VMEM((HEADS, head_pad, width), BF16),
             pltpu.VMEM((n, 2, width), BF16),
-            pltpu.VMEM((n, 1, width), F32),
+            pltpu.VMEM((n, 2, -(-width // 256) * 128), BF16),
             pltpu.VMEM((rows, width), F32),
             pltpu.VMEM((rows, width), F32),
             pltpu.VMEM((HEADS, rows, pack), BF16),
             pltpu.VMEM((n, rows, pack), BF16),
             pltpu.VMEM((n * rows, head_pad), BF16),
             pltpu.VMEM((n * rows, head_pad), BF16),
-            pltpu.VMEM((HEADS, rows, head_pad), BF16),
-            pltpu.VMEM((HEADS, rows, head_pad), BF16),
+            pltpu.VMEM((HEADS, fold_back, lane), BF16),
+            pltpu.VMEM((HEADS, fold_back, lane), BF16),
             pltpu.SemaphoreType.DMA((5,)),
             pltpu.SemaphoreType.DMA((HEADS,)),
             pltpu.SemaphoreType.DMA((n,)),
@@ -325,7 +393,7 @@
         counts, timestep, positions, pos_tab, time_tab,
         tokens, time_in, time_out.T, ada_weight, qkv_weight, out_weight,
     )
-    return result.astype(BF16)
+    return result
 
 
 def solution(mesh):

time: 35.4 us -> 34.2 us (0.966)
  other arithmetic: 1.59 us -> 0 us
  local copies, waits for them, and re-layouts: 0 us -> 1.55 us
  Pallas kernels: 33 us -> 31.8 us
    convert_element_type x1 -> x0, other arithmetic: 1.59 us -> none  [per_device(): return result.astype(BF16)]
    unnamed x0 -> x1, local copies, waits for them, and re-layouts: none -> 1.55 us
    pallas_call x1, Pallas kernels: 33 us -> 31.8 us  [per_device(): pl.pallas_call(functools.partial(block_kernel, n, rows, width, head), out...]
where the time goes in v4:
time: 34.2 us; the launch traced here: 34 us
  Pallas kernels  31.8 us (93%)
  local copies, waits for them, and re-layouts  1.55 us (5%)
  between operations  0.66 us (2%)
    pallas_call x1, Pallas kernels, per_device(): pl.pallas_call(functools.partial(block_kernel, n, rows, width, head), out...  31.8 us
    unnamed x1, local copies, waits for them, and re-layouts  1.55 us

profile of v4, /device:TPU:0, one launch (start us, length us, event | category | flops | bytes accessed | tf_op | source)
XLA Modules:
  0.0 34.0 jit_solution(14929353552601179715)
XLA Ops:
  0.7 31.8 %shard_map.109 = bf16[48,1152]{1,0:T(8,128)(2,1)} custom-call(s32[16]{0:T(128)} %counts.1, s32[1]{0:T(128)S(6)} %copy.13.tstep, s32[2,48]{1,0:T(2,128)} %pos.1, f32[2,1152]{1,0:T(2,128)} %constant.4.clone.pos_tab, f32[2,256]{1,0:T(2,128)} %constant.5.clone.time_tab, bf16[48,1152]{1,0:T(8,128)(2,1)} %tok_h.1, bf16[256,1152]{1,0:T(8,128)(2,1)} %tin_h.1, ...), custom_call_target="tpu_custom_call" | custom-call | tf_op jit(solution)/shard_map/pallas_call | solution.py:356
  32.5 1.6 %copy.14 = bf16[48,1152]{1,0:T(8,128)(2,1)} copy(bf16[48,1152]{1,0:T(8,128)(2,1)} %shard_map.109) | data formatting | bytes 221184

commit v5 on v4

--- a/solution.py
+++ b/solution.py
@@ -62,7 +62,7 @@
     tok_h, tin_h, tout_h, ada_h, qkv_h, ow_h,
     out,
     tok, tin, tout, ada, qkv, ow, mods, gates, xin_s, norm_s, send, got, kbuf, vbuf, att, back,
-    lsem, wsem, msend, mrecv, gsend, grecv, psend, precv, asend, arecv,
+    done, osem, lsem, wsem, msend, mrecv, gsend, grecv, psend, precv, asend, arecv,
 ):
     me = lax.axis_index("patch")
     my_head = lax.rem(me, HEADS)
@@ -319,14 +319,23 @@
         ],
         axis=1,
     ).astype(BF16)
-    projected = dot(attended, ow[...].reshape(HEADS * ow.shape[1], width))
+    weight = ow[...].reshape(HEADS * ow.shape[1], width)
     valid = (lax.broadcasted_iota(jnp.int32, (rows, 1), 0) < counts[me]).astype(F32)
-    out[...] = (xin_s[...] + gate * projected * valid).astype(BF16)
+    cut = width // 256 * 128
+    stores = []
+    for i, cols in enumerate([slice(0, cut), slice(cut, width)]):
+        projected = dot(attended, weight[:, cols])
+        done[:, cols] = (xin_s[:, cols] + gate[:, cols] * projected * valid).astype(BF16)
+        stores.append(pltpu.make_async_copy(done.at[:, cols], out.at[:, cols], osem.at[i]))
+        stores[-1].start()
 
     @pl.loop(1, HEADS)
     def _(step):
         other = lax.rem(my_head + step, HEADS)
         att_copy(other, other, other).wait_send()
+
+    for store in stores:
+        store.wait()
 
 
 def tables(width, freq):
@@ -357,7 +366,7 @@
         functools.partial(block_kernel, n, rows, width, head),
         out_shape=jax.ShapeDtypeStruct((rows, width), BF16),
         in_specs=[smem, smem, vmem, vmem, vmem] + [hbm] * 6,
-        out_specs=vmem,
+        out_specs=hbm,
         scratch_shapes=[
             pltpu.VMEM(tokens.shape, BF16),
             pltpu.VMEM(time_in.shape, BF16),
@@ -375,6 +384,8 @@
             pltpu.VMEM((n * rows, head_pad), BF16),
             pltpu.VMEM((HEADS, fold_back, lane), BF16),
             pltpu.VMEM((HEADS, fold_back, lane), BF16),
+            pltpu.VMEM((rows, width), BF16),
+            pltpu.SemaphoreType.DMA((2,)),
             pltpu.SemaphoreType.DMA((5,)),
             pltpu.SemaphoreType.DMA((HEADS,)),
             pltpu.SemaphoreType.DMA((n,)),

time: 34.2 us -> 34.1 us (level)
  no operation moved by 1% of the time
where the time goes in v5:
time: 34.1 us; the launch traced here: 33.9 us
  Pallas kernels  31.6 us (93%)
  local copies, waits for them, and re-layouts  1.55 us (5%)
  between operations  0.66 us (2%)
    pallas_call x1, Pallas kernels, per_device(): pl.pallas_call(functools.partial(block_kernel, n, rows, width, head), out...  31.6 us
    unnamed x1, local copies, waits for them, and re-layouts  1.55 us

profile of v5, /device:TPU:0, one launch (start us, length us, event | category | flops | bytes accessed | tf_op | source)
XLA Modules:
  0.0 33.9 jit_solution(1978166422979844664)
XLA Ops:
  0.7 31.6 %shard_map.109 = bf16[48,1152]{1,0:T(8,128)(2,1)} custom-call(s32[16]{0:T(128)} %counts.1, s32[1]{0:T(128)S(6)} %copy.13.tstep, s32[2,48]{1,0:T(2,128)} %pos.1, f32[2,1152]{1,0:T(2,128)} %constant.4.clone.pos_tab, f32[2,256]{1,0:T(2,128)} %constant.5.clone.time_tab, bf16[48,1152]{1,0:T(8,128)(2,1)} %tok_h.1, bf16[256,1152]{1,0:T(8,128)(2,1)} %tin_h.1, ...), custom_call_target="tpu_custom_call" | custom-call | tf_op jit(solution)/shard_map/pallas_call | solution.py:365
  32.3 1.6 %copy.14 = bf16[48,1152]{1,0:T(8,128)(2,1)} copy(bf16[48,1152]{1,0:T(8,128)(2,1)} %shard_map.109) | data formatting | bytes 221184
